TPU v7x, 256 devices: a whole 4x4x8 slice. The times are simulated.
256 devices in a mesh: seq: 64 (over z, y, core), rep: 4 (over x).
Axes of the slice: x: 4, y: 4, z: 8, core: 2. Of those that a mesh axis runs over, the one named last changes fastest.
Arguments:
- inputs: bfloat16 [4, 8192, 1024], P('rep', 'seq'), may hold values from -6 to 6
- weight_t: bfloat16 [3072, 1024], P('seq', 'rep'), may hold values from -0.1875 to 0.1875
- states: float32 [4, 8192, 1024], P('rep', 'seq'), may hold values from -0.9 to 0.9
- doc_ids: int32 [4, 8192], P('rep', 'seq'), may hold values from 0 to 31, never falling along the last dimension, each value on 1 to 512 neighbouring positions
- recur: float32 [3, 1024], replicated, may hold values from -1 to 1
- bias: float32 [3, 1024], replicated, may hold values from -8 to 3, as said below
- out_grad: bfloat16 [4, 8192, 1024], P('rep', 'seq'), may hold values from -6 to 6
Outputs:
- input_grad: bfloat16 [4, 8192, 1024], P('rep', 'seq')
- weight_grad: float32 [3072, 1024], P('seq', 'rep')
- param_grad: float32 [6, 1024], replicated
Inputs may be any that keep to these rules, and one draw needn't show every extreme that they name: `doc_ids`: within each sequence the numbers never fall; every document has 1 to 512 tokens, and some document has exactly 512. `bias`: row 0 lies between -8 and -1, rows 1 and 2 between -3 and 3.
All inputs are finite; a program needn't handle non-finite values.
Results may differ from a plain program's by a relative error of at most 0.0095.
Values may be sent and summed in bfloat16 or wider, within the bound.
No kernel may reach another device: no remote copies, remote signals or barrier semaphores. Data moves between devices by JAX's collectives and lax.ppermute only.
A program may use at most 128 MiB of HBM per device.

v0:
```python
import functools
import math
import jax
import jax.numpy as jnp
from jax import lax
from jax.sharding import Mesh
from jax.sharding import PartitionSpec as P

SEQ = ("seq_0", "seq_1", "seq_2")
SEQ_REP = ("seq_0", "seq_1", "seq_2", "rep")


def copy_for_each(x, axis):
    copies = jnp.broadcast_to(x, (lax.axis_size(axis), *x.shape))
    return lax.all_to_all(copies, axis, split_axis=0, concat_axis=0, tiled=True)


def joined_along(parts, dim):
    dims = list(parts.shape[1:])
    dims[dim] *= parts.shape[0]
    return jnp.moveaxis(parts, 0, dim).reshape(dims)


def collect(x, axis, dim):
    parts = copy_for_each(x, axis)
    return joined_along(parts, dim)


def shifted(block, axis, distance):
    devices = range(lax.axis_size(axis))
    route = [(i - distance, i) for i in devices if i - distance in devices]
    return lax.ppermute(block, axis, route)


def gathered_once(x, axis):
    leaves = jax.tree.leaves(x)
    sequence = sorted(range(len(leaves)), key=lambda k: -leaves[k].size)
    width = (1, *leaves[sequence[0]].shape)[-1]
    lines = [
        jnp.pad(leaves[k].reshape(-1), (0, -leaves[k].size % width)).reshape(-1, width)
        for k in sequence
    ]
    both, at, found = (copy_for_each(jnp.concatenate(lines), axis), 0, {})
    for k, line in zip(sequence, lines):
        piece = both[:, at : at + len(line)].reshape(len(both), -1)
        found[k] = piece[:, : leaves[k].size].reshape(-1, *leaves[k].shape)
        at += len(line)
    numbers = iter(range(len(leaves)))
    return jax.tree.map(lambda _: found[next(numbers)], x)


def combined_pairwise(pieces, combine):
    while len(jax.tree.leaves(pieces)[0]) > 1:
        pieces = jax.vmap(combine)(
            *(jax.tree.map(lambda part: part[side::2], pieces) for side in (0, 1))
        )
    return jax.tree.map(lambda part: part[0], pieces)


def carried_in(x, axis, combine, identity):
    count, here = (lax.axis_size(axis), lax.axis_index(axis))
    passed = jnp.arange(count) > here

    def kept(part, zero, own):
        part = jnp.where(
            passed.reshape(-1, *(1 for _ in own.shape)), part, jnp.asarray(zero, own.dtype)
        )
        return part[::-1]

    pieces = gathered_once(x, axis)
    return combined_pairwise(jax.tree.map(kept, pieces, identity, x), combine)


def split_up(x, dim, count):
    before, after = (x.shape[:dim], x.shape[dim + 1 :])
    return jnp.moveaxis(x.reshape(*before, count, -1, *after), dim, 0)


def sum_at_owner(x, axis, dim):
    parts = split_up(x, dim, lax.axis_size(axis))
    arrived = lax.all_to_all(parts, axis, split_axis=0, concat_axis=0, tiled=True)
    return arrived.astype(jnp.float32).sum(axis=0)


def by_axis(x, axes):
    return functools.reduce(lax.psum, axes, x)


def compose(earlier, later):
    return (later[0] * earlier[0], later[1] + later[0] * earlier[1])


def local(inputs, weight_t, states, doc_ids, recur, bias, out_grad):
    feats = inputs[0]
    hidden_now = states[0]
    ids_float = doc_ids[0].astype(jnp.float32)
    count = feats.shape[0]
    width = hidden_now.shape[1]
    columns = collect(weight_t, "rep", 1)
    contract_last = (((1,), (1,)), ((), ()))
    full_weight = lax.all_gather(columns, SEQ, axis=0, tiled=True)
    preact = lax.dot_general(feats, full_weight, contract_last, preferred_element_type=jnp.float32)
    tail_state, tail_id = shifted((hidden_now[-1:], ids_float[-1:]), SEQ, 1)
    first_same = jnp.where(
        (ids_float[0] == tail_id[0]) & (lax.axis_index(SEQ) > 0), 1.0, 0.0
    ).astype(jnp.float32)
    same = jnp.concatenate(
        [first_same[None], (ids_float[1:] == ids_float[:-1]).astype(jnp.float32)]
    )
    prior = jnp.concatenate([tail_state, hidden_now[:-1]], 0) * same[:, None]
    gate_z = jax.nn.sigmoid(preact[:, :width] + recur[0] * prior + bias[0])
    gate_r = jax.nn.sigmoid(preact[:, width : 2 * width] + recur[1] * prior + bias[1])
    gate_c = jnp.tanh(preact[:, 2 * width :] + recur[2] * gate_r * prior + bias[2])
    jacobian = same[:, None] * (
        1.0
        - gate_z
        + (gate_c - prior) * gate_z * (1.0 - gate_z) * recur[0]
        + gate_z
        * (1.0 - gate_c * gate_c)
        * recur[2]
        * (gate_r + prior * gate_r * (1.0 - gate_r) * recur[1])
    )
    upstream = out_grad[0].astype(jnp.float32)
    next_row = shifted(jacobian[:1], SEQ, -1)
    factor = jnp.concatenate([jacobian[1:], next_row], 0)
    product, local_adj = lax.associative_scan(compose, (factor, upstream), reverse=True, axis=0)
    ones_row = jnp.ones((1, width), jnp.float32)
    zeros_row = jnp.zeros((1, width), jnp.float32)
    _, entering = carried_in((product[:1], local_adj[:1]), SEQ, compose, (ones_row, zeros_row))
    adjoint = local_adj + product * entering
    grad_z = adjoint * (gate_c - prior) * gate_z * (1.0 - gate_z)
    grad_c = adjoint * gate_z * (1.0 - gate_c * gate_c)
    grad_r = grad_c * recur[2] * prior * gate_r * (1.0 - gate_r)
    grad_pre = jnp.concatenate([grad_z, grad_r, grad_c], 1).astype(jnp.bfloat16)
    input_grad = jnp.dot(grad_pre, full_weight, preferred_element_type=jnp.float32)
    tokens_all = count * inputs.shape[0] * lax.axis_size(SEQ) * lax.axis_size("rep")
    normal_factor = 1.0 / math.sqrt(tokens_all)
    row_share = lax.psum_scatter(
        lax.dot_general(
            grad_pre, feats, (((0,), (0,)), ((), ())), preferred_element_type=jnp.float32
        ),
        SEQ,
        scatter_dimension=0,
        tiled=True,
    )
    weight_grad = sum_at_owner(row_share.astype(jnp.bfloat16), "rep", 1) * normal_factor
    stats = jnp.stack(
        [
            grad_z.sum(0),
            grad_r.sum(0),
            grad_c.sum(0),
            (grad_z * prior).sum(0),
            (grad_r * prior).sum(0),
            (grad_c * gate_r * prior).sum(0),
        ]
    )
    param_grad = by_axis(stats, SEQ_REP) * normal_factor
    return (input_grad.astype(jnp.bfloat16)[None], weight_grad, param_grad)


def solution(mesh):
    torus = Mesh(
        mesh.devices.reshape(8, 4, 2, mesh.shape["rep"]), ("seq_0", "seq_1", "seq_2", "rep")
    )
    in_specs = (
        P("rep", SEQ, None),
        P(SEQ, "rep"),
        P("rep", SEQ, None),
        P("rep", SEQ),
        P(),
        P(),
        P("rep", SEQ, None),
    )
    out_specs = (P("rep", SEQ, None), P(SEQ, "rep"), P())
    return jax.shard_map(local, mesh=torus, in_specs=in_specs, out_specs=out_specs, check_vma=False)
```

profile of v0, /device:TPU:2, one launch (start us, length us, event | category | flops | bytes accessed | tf_op | source)
XLA Modules:
  0.0 406.0 jit_solution(11852315016412689403)
XLA Ops:
  8.1 9.0 %all_to_all.15 = bf16[4,48,256]{2,1,0:T(8,128)(2,1)S(1)} all-to-all(bf16[4,48,256]{2,1,0:T(8,128)(2,1)S(1)} %broadcast_in_dim.35), channel_id=1, replica_groups=mesh['seq_0'=8,'seq_1'=4,'seq_2'=2,'rep'=4] {'rep'}, dimensions={0} | all-to-all | bytes 196608 | tf_op jit(solution)/shard_map/all_to_all | solution.py:15
  21.6 3.6 collective-permute-start.1
  30.4 70.1 %all-gather.2.cloned.1.call-done = bf16[3072,1024]{1,0:T(8,128)(2,1)} async-done(((bf16[48,1024]{1,0:T(8,128)(2,1)}), bf16[3072,1024]{1,0:T(8,128)(2,1)}) %all-gather.2.cloned.1.call-update) | async-done | bytes 6291472 | tf_op jit(solution)/shard_map/all_gather | solution.py:101
  100.5 5.0 %fusion.16 = f32[128,3072]{1,0:T(8,128)S(1)} fusion(bf16[3072,1024]{1,0:T(8,128)(2,1)} %all-gather.2.cloned.1.call-done, bf16[1,128,1024]{2,1,0:T(8,128)(2,1)S(1)} %copy-done), kind=kOutput, calls=%fused_computation.39 | convolution fusion | flops 805306368 | bytes 8126464 | tf_op jit(solution)/shard_map/dot_general | solution.py:102
  111.3 4.3 %slice.416 = f32[64,1024]{1,0:T(8,128)} reverse(f32[64,1024]{1,0:T(8,128)} %slice.415), dimensions={0} | reverse | bytes 524288 | tf_op jit(solution)/shard_map/slice | solution.py:126
  115.6 4.3 %slice.420 = f32[64,1024]{1,0:T(8,128)} reverse(f32[64,1024]{1,0:T(8,128)} %slice.419), dimensions={0} | reverse | bytes 524288 | tf_op jit(solution)/shard_map/slice | solution.py:126
  120.0 4.3 %slice.391 = f32[63,1024]{1,0:T(8,128)} reverse(f32[63,1024]{1,0:T(8,128)} %slice.390), dimensions={0} | reverse | bytes 516096 | tf_op jit(solution)/shard_map/slice | solution.py:126
  125.5 4.3 %slice.418 = f32[64,1024]{1,0:T(8,128)} reverse(f32[64,1024]{1,0:T(8,128)} %slice.417), dimensions={0} | reverse | bytes 524288 | tf_op jit(solution)/shard_map/slice | solution.py:126
  129.8 2.5 slice.424
  169.5 2.5 slice.414
  184.8 2.6 pad.112
  187.5 2.6 pad.113
  191.9 9.2 %all-to-all-start.1 = ((f32[64,2,1024]{2,1,0:T(2,128)}), f32[64,2,1024]{2,1,0:T(2,128)}, u32[]{:S(2)}, u32[]{:S(2)}) async-start(f32[64,2,1024]{2,1,0:T(2,128)} %broadcast_in_dim.37), calls=%async_computation.1 | async-start | bytes 1048576 | tf_op jit(solution)/shard_map/all_to_all | solution.py:15
  204.1 3.4 rev.5
  207.6 10.9 %all-to-all-done.1 = f32[64,2,1024]{2,1,0:T(2,128)} async-done(((f32[64,2,1024]{2,1,0:T(2,128)}), f32[64,2,1024]{2,1,0:T(2,128)}, u32[]{:S(2)}, u32[]{:S(2)}) %all-to-all-start.1) | async-done | bytes 524320 | tf_op jit(solution)/shard_map/all_to_all | solution.py:15
  223.1 6.4 %fusion.13 = f32[3072,1024]{1,0:T(8,128)} fusion(bf16[128,1024]{1,0:T(8,128)(2,1)S(1)} %get-tuple-element.11, bf16[128,1024]{1,0:T(8,128)(2,1)S(1)} %get-tuple-element.10, bf16[128,1024]{1,0:T(8,128)(2,1)S(1)} %get-tuple-element.9, bf16[1,128,1024]{2,1,0:T(8,128)(2,1)S(1)} %copy-done), kind=kOutput, calls=%fused_computation.32 | convolution fusion | flops 807665664 | bytes 13631488 | tf_op jit(solution)/shard_map/dot_general | solution.py:139
  229.5 28.7 %psum.28 = f32[6,1024]{1,0:T(8,128)S(1)} all-reduce(f32[6,1024]{1,0:T(8,128)S(1)} %stack.27), channel_id=1, replica_groups=mesh['seq_0'=8,'seq_1'=4,'seq_2'=2,'rep'=4] {'seq_0'}, use_global_device_ids=true, to_apply=%region_8.9 | all-reduce | flops 6144 | bytes 49152 | tf_op jit(solution)/shard_map/psum | solution.py:86
  258.3 16.3 %psum.29 = f32[6,1024]{1,0:T(8,128)S(1)} all-reduce(f32[6,1024]{1,0:T(8,128)S(1)} %psum.28), channel_id=1, replica_groups=mesh['seq_0'=8,'seq_1'=4,'seq_2'=2,'rep'=4] {'seq_1'}, use_global_device_ids=true, to_apply=%region_9.10 | all-reduce | flops 6144 | bytes 49152 | tf_op jit(solution)/shard_map/psum | solution.py:86
  274.6 3.4 psum.30
  278.0 14.1 %psum.31 = f32[6,1024]{1,0:T(8,128)S(1)} all-reduce(f32[6,1024]{1,0:T(8,128)S(1)} %psum.30), channel_id=1, replica_groups=mesh['seq_0'=8,'seq_1'=4,'seq_2'=2,'rep'=4] {'rep'}, use_global_device_ids=true, to_apply=%region_11.12 | all-reduce | flops 6144 | bytes 49152 | tf_op jit(solution)/shard_map/psum | solution.py:86
  292.1 4.6 %fusion = bf16[1,128,1024]{2,1,0:T(8,128)(2,1)} fusion(bf16[3072,1024]{1,0:T(8,128)(2,1)} %all-gather.2.cloned.1.call-done, bf16[128,1024]{1,0:T(8,128)(2,1)S(1)} %copy-done.9, bf16[128,1024]{1,0:T(8,128)(2,1)S(1)} %copy-done.7, bf16[128,1024]{1,0:T(8,128)(2,1)S(1)} %copy-done.5), kind=kOutput, calls=%fused_computation.1 | convolution fusion | flops 807796736 | bytes 7340032 | tf_op jit(solution)/shard_map/dot_general | solution.py:135
  296.7 91.0 %reduce-scatter.2.cloned.1.call-done = f32[48,1024]{1,0:T(8,128)} async-done(((f32[3072,1024]{1,0:T(8,128)}), f32[48,1024]{1,0:T(8,128)}) %reduce-scatter.2.cloned.1.call-update) | async-done | bytes 196624 | tf_op jit(solution)/shard_map/reduce_scatter | solution.py:138
  389.3 4.8 %all-to-all-start.2 = ((bf16[4,48,256]{2,1,0:T(8,128)(2,1)}), bf16[4,48,256]{2,1,0:T(8,128)(2,1)S(1)}, u32[]{:S(2)}, u32[]{:S(2)}) async-start(bf16[4,48,256]{2,1,0:T(8,128)(2,1)} %bitcast.45), calls=%async_computation.3 | async-start | bytes 196608 | tf_op jit(solution)/shard_map/all_to_all | solution.py:81
  394.7 3.7 all-to-all-done.2
  (230 shorter events, 77.7 us)
Async XLA Ops:
  7.2 93.3 %copy-start = (bf16[1,128,1024]{2,1,0:T(8,128)(2,1)S(1)}, bf16[1,128,1024]{2,1,0:T(8,128)(2,1)}, u32[]{:S(2)}) copy-start(bf16[1,128,1024]{2,1,0:T(8,128)(2,1)} %param.7) | copy-start | bytes 786436
  7.2 21.7 %copy-start.12 = (f32[1,128,1024]{2,1,0:T(8,128)S(1)}, f32[1,128,1024]{2,1,0:T(8,128)}, u32[]{:S(2)}) copy-start(f32[1,128,1024]{2,1,0:T(8,128)} %param.9) | copy-start | bytes 1572868
  7.2 93.3 %all-gather.2.cloned.1.call-start = ((), (), s32[]{:S(2)}) async-start(), calls=%async_computation.4 | async-start | bytes 6389760 | tf_op jit(solution)/shard_map/all_gather | solution.py:101
  18.9 10.0 %collective-permute-start = (f32[1]{0:T(128)}, f32[1]{0:T(128)}, u32[]{:S(2)}, u32[]{:S(2)}) collective-permute-start(f32[1]{0:T(128)} %bitcast.3), channel_id=1, source_target_pairs={{0,4},{4,8},{8,12},{12,16},{16,20},{20,24},{24,28},{28,32},{32,36}... | collective-permute-start | bytes 20 | tf_op jit(solution)/shard_map/ppermute | solution.py:32
  21.6 83.9 %collective-permute-start.1 = (f32[1,1024]{1,0:T(1,128)S(1)}, f32[1,1024]{1,0:T(1,128)S(1)}, u32[]{:S(2)}, u32[]{:S(2)}) collective-permute-start(f32[1,1024]{1,0:T(1,128)S(1)} %slice_bitcast_fusion.2), channel_id=1, source_target_pairs={{0,4},{4,8},{8,12},{12,16},{16,20},{20,24},{24,28},{28,32},{32,36}... | collective-permute-start | bytes 12296 | tf_op jit(solution)/shard_map/ppermute | solution.py:32
  26.1 79.3 %copy-start.16 = (f32[1,1024]{1,0:T(1,128)}, f32[1,1024]{1,0:T(1,128)S(1)}, u32[]{:S(2)}) copy-start(f32[1,1024]{1,0:T(1,128)S(1)} %get-tuple-element.58) | copy-start | bytes 12292
  26.1 79.3 %copy-start.18 = (f32[1,1024]{1,0:T(1,128)}, f32[1,1024]{1,0:T(1,128)S(1)}, u32[]{:S(2)}) copy-start(f32[1,1024]{1,0:T(1,128)S(1)} %get-tuple-element.59) | copy-start | bytes 12292
  26.1 79.3 %copy-start.20 = (f32[1,1024]{1,0:T(1,128)}, f32[1,1024]{1,0:T(1,128)S(1)}, u32[]{:S(2)}) copy-start(f32[1,1024]{1,0:T(1,128)S(1)} %get-tuple-element.60) | copy-start | bytes 12292
  27.0 78.5 %copy-start.22 = (f32[1,1024]{1,0:T(1,128)}, f32[1,1024]{1,0:T(1,128)S(1)}, u32[]{:S(2)}) copy-start(f32[1,1024]{1,0:T(1,128)S(1)} %get-tuple-element.55) | copy-start | bytes 12292
  27.0 78.5 %copy-start.24 = (f32[1,1024]{1,0:T(1,128)}, f32[1,1024]{1,0:T(1,128)S(1)}, u32[]{:S(2)}) copy-start(f32[1,1024]{1,0:T(1,128)S(1)} %get-tuple-element.56) | copy-start | bytes 12292
  27.0 78.5 %copy-start.26 = (f32[1,1024]{1,0:T(1,128)}, f32[1,1024]{1,0:T(1,128)S(1)}, u32[]{:S(2)}) copy-start(f32[1,1024]{1,0:T(1,128)S(1)} %get-tuple-element.57) | copy-start | bytes 12292
  30.4 75.1 %copy-start.39 = (f32[128]{0:T(128)}, f32[128]{0:T(128)S(1)}, u32[]{:S(2)}) copy-start(f32[128]{0:T(128)S(1)} %pad_maximum_fusion.17) | copy-start | bytes 1540
  106.3 18.0 %collective-permute-start.2 = (f32[1,1024]{1,0:T(1,128)S(1)}, f32[1,1024]{1,0:T(1,128)S(1)}, u32[]{:S(2)}, u32[]{:S(2)}) collective-permute-start(f32[1,1024]{1,0:T(1,128)S(1)} %slice.515), channel_id=1, source_target_pairs={{4,0},{8,4},{12,8},{16,12},{20,16},{24,20},{28,24},{32,28},{36,32}... | collective-permute-start | bytes 12296 | tf_op jit(solution)/shard_map/ppermute | solution.py:32
  159.9 14.4 %copy-start.15 = (f32[3,1024]{1,0:T(4,128)S(1)}, f32[3,1024]{1,0:T(4,128)}, u32[]{:S(2)}) copy-start(f32[3,1024]{1,0:T(4,128)} %slice.446) | copy-start | bytes 36868
  168.3 9.2 %copy-start.13 = (f32[15,1024]{1,0:T(8,128)S(1)}, f32[15,1024]{1,0:T(8,128)}, u32[]{:S(2)}) copy-start(f32[15,1024]{1,0:T(8,128)} %slice.432) | copy-start | bytes 184324
  168.3 9.2 %copy-start.14 = (f32[15,1024]{1,0:T(8,128)S(1)}, f32[15,1024]{1,0:T(8,128)}, u32[]{:S(2)}) copy-start(f32[15,1024]{1,0:T(8,128)} %slice.430) | copy-start | bytes 184324
  168.9 8.5 %copy-start.35 = (f32[1,1024]{1,0:T(1,128)S(1)}, f32[1,1024]{1,0:T(1,128)}, u32[]{:S(2)}) copy-start(f32[1,1024]{1,0:T(1,128)} %slice.518) | copy-start | bytes 12292
  168.9 8.6 %copy-start.34 = (f32[1,1024]{1,0:T(1,128)S(1)}, f32[1,1024]{1,0:T(1,128)}, u32[]{:S(2)}) copy-start(f32[1,1024]{1,0:T(1,128)} %slice.539) | copy-start | bytes 12292
  191.9 26.6 %all-to-all-start.1 = ((f32[64,2,1024]{2,1,0:T(2,128)}), f32[64,2,1024]{2,1,0:T(2,128)}, u32[]{:S(2)}, u32[]{:S(2)}) async-start(f32[64,2,1024]{2,1,0:T(2,128)} %broadcast_in_dim.37), calls=%async_computation.1 | async-start | bytes 1048576 | tf_op jit(solution)/shard_map/all_to_all | solution.py:15
  201.1 186.7 %reduce-scatter.2.cloned.1.call-start = ((), (), s32[]{:S(2)}) async-start(), calls=%async_computation.5 | async-start | bytes 12779520 | tf_op jit(solution)/shard_map/reduce_scatter | solution.py:138
  229.5 62.6 %copy-start.5 = (bf16[128,1024]{1,0:T(8,128)(2,1)S(1)}, bf16[128,1024]{1,0:T(8,128)(2,1)}, u32[]{:S(2)}) copy-start(bf16[128,1024]{1,0:T(8,128)(2,1)} %copy-done.4) | copy-start | bytes 786436
  229.5 62.6 %copy-start.7 = (bf16[128,1024]{1,0:T(8,128)(2,1)S(1)}, bf16[128,1024]{1,0:T(8,128)(2,1)}, u32[]{:S(2)}) copy-start(bf16[128,1024]{1,0:T(8,128)(2,1)} %copy-done.6) | copy-start | bytes 786436
  229.5 62.6 %copy-start.9 = (bf16[128,1024]{1,0:T(8,128)(2,1)S(1)}, bf16[128,1024]{1,0:T(8,128)(2,1)}, u32[]{:S(2)}) copy-start(bf16[128,1024]{1,0:T(8,128)(2,1)} %copy-done.8) | copy-start | bytes 786436
  389.3 9.2 %all-to-all-start.2 = ((bf16[4,48,256]{2,1,0:T(8,128)(2,1)}), bf16[4,48,256]{2,1,0:T(8,128)(2,1)S(1)}, u32[]{:S(2)}, u32[]{:S(2)}) async-start(bf16[4,48,256]{2,1,0:T(8,128)(2,1)} %bitcast.45), calls=%async_computation.3 | async-start | bytes 196608 | tf_op jit(solution)/shard_map/all_to_all | solution.py:81
  (24 other events, 39.1 us)
Sparse Core Ops, SparseCore 0:
  17.8 82.6 all-gather.1
  229.6 158.0 reduce-scatter.1
where the time goes:
time: 410 us; the launch traced here: 406 us
  waiting for transfers between devices  176 us (43%)
  local copies, waits for them, and re-layouts  75.4 us (18%)
  blocking collectives  71.5 us (17%)
  other arithmetic  30 us (7%)
  starting transfers between devices  21 us (5%)
  between operations  16.4 us (4%)
  matrix products  16 us (4%)
    reduce_scatter x1, waiting for transfers between devices, local(): lax.psum_scatter(lax.dot_general(grad_pre, feats, (((0,), (0,)), ((), ())...  91 us
    all_gather x1, waiting for transfers between devices, local(): full_weight = lax.all_gather(columns, SEQ, axis=0, tiled=True)  70.1 us
    psum x4, blocking collectives, by_axis(): return functools.reduce(lax.psum, axes, x)  62.5 us
    slice x49, local copies, waits for them, and re-layouts, local(): lax.associative_scan(compose, (factor, upstream), reverse=True, axis=0)  55.3 us
    all_to_all x1, waiting for transfers between devices, copy_for_each(): return lax.all_to_all(copies, axis, split_axis=0, concat_axis=0, tiled=True)  10.9 us
    mul x16, other arithmetic, compose(): return (later[0] * earlier[0], later[1] + later[0] * earlier[1])  10.4 us
    all_to_all x1, starting transfers between devices, copy_for_each(): return lax.all_to_all(copies, axis, split_axis=0, concat_axis=0, tiled=True)  9.17 us
    all_to_all x1, blocking collectives, copy_for_each(): return lax.all_to_all(copies, axis, split_axis=0, concat_axis=0, tiled=True)  8.96 us
  transfers between devices with their start and end apart: 7, of which 4 were waited for; matrix products, arithmetic and copies ran while one was open for 9% of the time, Pallas kernels for 0%

commit v1 on v0

--- a/solution.py
+++ b/solution.py
@@ -98,7 +98,8 @@
     width = hidden_now.shape[1]
     columns = collect(weight_t, "rep", 1)
     contract_last = (((1,), (1,)), ((), ()))
-    full_weight = lax.all_gather(columns, SEQ, axis=0, tiled=True)
+    stack = jnp.stack([columns] * lax.axis_size(SEQ))
+    full_weight = jnp.concatenate(lax.all_to_all(stack, SEQ, 0, 0), axis=0)
     preact = lax.dot_general(feats, full_weight, contract_last, preferred_element_type=jnp.float32)
     tail_state, tail_id = shifted((hidden_now[-1:], ids_float[-1:]), SEQ, 1)
     first_same = jnp.where(

time: 410 us -> 481 us (1.17)
  waiting for transfers between devices: 176 us -> 237 us
  starting transfers between devices: 21 us -> 32 us
    all_to_all x0 -> x1, waiting for transfers between devices: none -> 133 us  [local(): full_weight = jnp.concatenate(lax.all_to_all(stack, SEQ, 0, 0), axis=0)]
    all_gather x1 -> x0, waiting for transfers between devices: 70.1 us -> none  [local(): full_weight = lax.all_gather(columns, SEQ, axis=0, tiled=True)]
    all_to_all x0 -> x1, starting transfers between devices: none -> 12.5 us  [local(): full_weight = jnp.concatenate(lax.all_to_all(stack, SEQ, 0, 0), axis=0)]
  transfers between devices with their start and end apart: 7 -> 7, of which waited for: 4 -> 4; matrix products, arithmetic and copies ran while one was open for 9% -> 7% of each run, Pallas kernels for 0% -> 0%
where the time goes in v1:
time: 481 us; the launch traced here: 477 us
  waiting for transfers between devices  237 us (49%)
  local copies, waits for them, and re-layouts  75.8 us (16%)
  blocking collectives  72 us (15%)
  starting transfers between devices  32 us (7%)
  other arithmetic  28.3 us (6%)
  between operations  16.5 us (3%)
  matrix products  15.9 us (3%)
    all_to_all x1, waiting for transfers between devices, local(): full_weight = jnp.concatenate(lax.all_to_all(stack, SEQ, 0, 0), axis=0)  133 us
    reduce_scatter x1, waiting for transfers between devices, local(): lax.psum_scatter(lax.dot_general(grad_pre, feats, (((0,), (0,)), ((), ())...  89.7 us
    psum x4, blocking collectives, by_axis(): return functools.reduce(lax.psum, axes, x)  63 us
    slice x49, local copies, waits for them, and re-layouts, local(): lax.associative_scan(compose, (factor, upstream), reverse=True, axis=0)  55.3 us
    all_to_all x1, starting transfers between devices, local(): full_weight = jnp.concatenate(lax.all_to_all(stack, SEQ, 0, 0), axis=0)  12.5 us
    all_to_all x1, waiting for transfers between devices, copy_for_each(): return lax.all_to_all(copies, axis, split_axis=0, concat_axis=0, tiled=True)  10.9 us
    mul x16, other arithmetic, compose(): return (later[0] * earlier[0], later[1] + later[0] * earlier[1])  10.4 us
  transfers between devices with their start and end apart: 7, of which 4 were waited for; matrix products, arithmetic and copies ran while one was open for 7% of the time, Pallas kernels for 0%

profile of v1, /device:TPU:2, one launch (start us, length us, event | category | flops | bytes accessed | tf_op | source)
XLA Modules:
  0.0 477.3 jit_solution(725182742763746214)
XLA Ops:
  8.0 9.0 %all_to_all.20 = bf16[4,48,256]{2,1,0:T(8,128)(2,1)S(1)} all-to-all(bf16[4,48,256]{2,1,0:T(8,128)(2,1)S(1)} %broadcast_in_dim.35), channel_id=1, replica_groups=mesh['seq_0'=8,'seq_1'=4,'seq_2'=2,'rep'=4] {'rep'}, dimensions={0} | all-to-all | bytes 196608 | tf_op jit(solution)/shard_map/all_to_all | solution.py:15
  16.9 3.5 stack.24
  20.4 12.5 %all-to-all-start.1 = ((bf16[64,48,1024]{2,1,0:T(8,128)(2,1)}), bf16[64,48,1024]{2,1,0:T(8,128)(2,1)}, u32[]{:S(2)}, u32[]{:S(2)}) async-start(bf16[64,48,1024]{2,1,0:T(8,128)(2,1)} %stack.24), calls=%async_computation.1 | async-start | bytes 12582912 | tf_op jit(solution)/shard_map/all_to_all | solution.py:102
  36.0 3.0 collective-permute-start.1
  41.6 132.6 %all-to-all-done.1 = bf16[64,48,1024]{2,1,0:T(8,128)(2,1)} async-done(((bf16[64,48,1024]{2,1,0:T(8,128)(2,1)}), bf16[64,48,1024]{2,1,0:T(8,128)(2,1)}, u32[]{:S(2)}, u32[]{:S(2)}) %all-to-all-start.1) | async-done | bytes 6291488 | tf_op jit(solution)/shard_map/all_to_all | solution.py:102
  174.2 5.0 %fusion.16 = f32[128,3072]{1,0:T(8,128)S(1)} fusion(bf16[3072,1024]{1,0:T(8,128)(2,1)} %bitcast.9, bf16[1,128,1024]{2,1,0:T(8,128)(2,1)S(1)} %copy-done), kind=kOutput, calls=%fused_computation.39 | convolution fusion | flops 805306368 | bytes 8126464 | tf_op jit(solution)/shard_map/dot_general | solution.py:103
  185.0 4.3 slice.416
  189.4 4.3 slice.420
  193.7 4.4 slice.391
  199.2 4.3 slice.418
  258.5 2.7 pad.112
  261.2 2.7 pad.113
  265.6 7.8 %all-to-all-start.2 = ((f32[64,2,1024]{2,1,0:T(2,128)}), f32[64,2,1024]{2,1,0:T(2,128)}, u32[]{:S(2)}, u32[]{:S(2)}) async-start(f32[64,2,1024]{2,1,0:T(2,128)} %broadcast_in_dim.37), calls=%async_computation.2 | async-start | bytes 1048576 | tf_op jit(solution)/shard_map/all_to_all | solution.py:15
  276.5 3.4 rev.5
  279.9 10.9 %all-to-all-done.2 = f32[64,2,1024]{2,1,0:T(2,128)} async-done(((f32[64,2,1024]{2,1,0:T(2,128)}), f32[64,2,1024]{2,1,0:T(2,128)}, u32[]{:S(2)}, u32[]{:S(2)}) %all-to-all-start.2) | async-done | bytes 524320 | tf_op jit(solution)/shard_map/all_to_all | solution.py:15
  295.4 6.4 %fusion.13 = f32[3072,1024]{1,0:T(8,128)} fusion(bf16[128,1024]{1,0:T(8,128)(2,1)S(1)} %get-tuple-element.11, bf16[128,1024]{1,0:T(8,128)(2,1)S(1)} %get-tuple-element.10, bf16[128,1024]{1,0:T(8,128)(2,1)S(1)} %get-tuple-element.9, bf16[1,128,1024]{2,1,0:T(8,128)(2,1)S(1)} %copy-done), kind=kOutput, calls=%fused_computation.32 | convolution fusion | flops 807665664 | bytes 13631488 | tf_op jit(solution)/shard_map/dot_general | solution.py:140
  301.8 28.7 %psum.28 = f32[6,1024]{1,0:T(8,128)S(1)} all-reduce(f32[6,1024]{1,0:T(8,128)S(1)} %stack.31), channel_id=1, replica_groups=mesh['seq_0'=8,'seq_1'=4,'seq_2'=2,'rep'=4] {'seq_0'}, use_global_device_ids=true, to_apply=%region_8.9 | all-reduce | flops 6144 | bytes 49152 | tf_op jit(solution)/shard_map/psum | solution.py:86
  330.6 16.3 %psum.29 = f32[6,1024]{1,0:T(8,128)S(1)} all-reduce(f32[6,1024]{1,0:T(8,128)S(1)} %psum.28), channel_id=1, replica_groups=mesh['seq_0'=8,'seq_1'=4,'seq_2'=2,'rep'=4] {'seq_1'}, use_global_device_ids=true, to_apply=%region_9.10 | all-reduce | flops 6144 | bytes 49152 | tf_op jit(solution)/shard_map/psum | solution.py:86
  346.9 3.4 psum.30
  350.3 14.6 %psum.31 = f32[6,1024]{1,0:T(8,128)S(1)} all-reduce(f32[6,1024]{1,0:T(8,128)S(1)} %psum.30), channel_id=1, replica_groups=mesh['seq_0'=8,'seq_1'=4,'seq_2'=2,'rep'=4] {'rep'}, use_global_device_ids=true, to_apply=%region_11.12 | all-reduce | flops 6144 | bytes 49152 | tf_op jit(solution)/shard_map/psum | solution.py:86
  364.9 4.5 fusion
  369.4 89.7 %reduce-scatter.2.cloned.1.call-done = f32[48,1024]{1,0:T(8,128)} async-done(((f32[3072,1024]{1,0:T(8,128)}), f32[48,1024]{1,0:T(8,128)}) %reduce-scatter.2.cloned.1.call-update) | async-done | bytes 196624 | tf_op jit(solution)/shard_map/reduce_scatter | solution.py:139
  460.7 4.8 %all-to-all-start.3 = ((bf16[4,48,256]{2,1,0:T(8,128)(2,1)}), bf16[4,48,256]{2,1,0:T(8,128)(2,1)S(1)}, u32[]{:S(2)}, u32[]{:S(2)}) async-start(bf16[4,48,256]{2,1,0:T(8,128)(2,1)} %bitcast.46), calls=%async_computation.4 | async-start | bytes 196608 | tf_op jit(solution)/shard_map/all_to_all | solution.py:81
  466.1 3.7 all-to-all-done.3
  (238 shorter events, 78.5 us)
Async XLA Ops:
  7.2 167.1 %copy-start = (bf16[1,128,1024]{2,1,0:T(8,128)(2,1)S(1)}, bf16[1,128,1024]{2,1,0:T(8,128)(2,1)}, u32[]{:S(2)}) copy-start(bf16[1,128,1024]{2,1,0:T(8,128)(2,1)} %param.7) | copy-start | bytes 786436
  20.4 12.5 %copy-start.44 = (s32[1,128]{1,0:T(1,128)S(1)}, s32[1,128]{1,0:T(1,128)}, u32[]{:S(2)}) copy-start(s32[1,128]{1,0:T(1,128)} %param.10) | copy-start | bytes 1540
  20.4 15.6 %copy-start.12 = (f32[1,128,1024]{2,1,0:T(8,128)S(1)}, f32[1,128,1024]{2,1,0:T(8,128)}, u32[]{:S(2)}) copy-start(f32[1,128,1024]{2,1,0:T(8,128)} %param.9) | copy-start | bytes 1572868
  20.4 18.7 %copy-start.40 = (f32[3,1024]{1,0:T(4,128)S(1)}, f32[3,1024]{1,0:T(4,128)}, u32[]{:S(2)}) copy-start(f32[3,1024]{1,0:T(4,128)} %param.12) | copy-start | bytes 36868
  20.4 18.7 %copy-start.41 = (f32[3,1024]{1,0:T(4,128)S(1)}, f32[3,1024]{1,0:T(4,128)}, u32[]{:S(2)}) copy-start(f32[3,1024]{1,0:T(4,128)} %param.11) | copy-start | bytes 36868
  20.4 18.7 %copy-start.13 = (bf16[1,128,1024]{2,1,0:T(8,128)(2,1)S(1)}, bf16[1,128,1024]{2,1,0:T(8,128)(2,1)}, u32[]{:S(2)}) copy-start(bf16[1,128,1024]{2,1,0:T(8,128)(2,1)} %param.13) | copy-start | bytes 786436
  20.4 153.8 %all-to-all-start.1 = ((bf16[64,48,1024]{2,1,0:T(8,128)(2,1)}), bf16[64,48,1024]{2,1,0:T(8,128)(2,1)}, u32[]{:S(2)}, u32[]{:S(2)}) async-start(bf16[64,48,1024]{2,1,0:T(8,128)(2,1)} %stack.24), calls=%async_computation.1 | async-start | bytes 12582912 | tf_op jit(solution)/shard_map/all_to_all | solution.py:102
  33.5 6.6 %collective-permute-start = (f32[1]{0:T(128)}, f32[1]{0:T(128)}, u32[]{:S(2)}, u32[]{:S(2)}) collective-permute-start(f32[1]{0:T(128)} %bitcast.3), channel_id=1, source_target_pairs={{0,4},{4,8},{8,12},{12,16},{16,20},{20,24},{24,28},{28,32},{32,36}... | collective-permute-start | bytes 20 | tf_op jit(solution)/shard_map/ppermute | solution.py:32
  36.0 143.2 %collective-permute-start.1 = (f32[1,1024]{1,0:T(1,128)S(1)}, f32[1,1024]{1,0:T(1,128)S(1)}, u32[]{:S(2)}, u32[]{:S(2)}) collective-permute-start(f32[1,1024]{1,0:T(1,128)S(1)} %slice_bitcast_fusion.2), channel_id=1, source_target_pairs={{0,4},{4,8},{8,12},{12,16},{16,20},{20,24},{24,28},{28,32},{32,36}... | collective-permute-start | bytes 12296 | tf_op jit(solution)/shard_map/ppermute | solution.py:32
  39.1 140.1 %copy-start.17 = (f32[1,1024]{1,0:T(1,128)}, f32[1,1024]{1,0:T(1,128)S(1)}, u32[]{:S(2)}) copy-start(f32[1,1024]{1,0:T(1,128)S(1)} %get-tuple-element.58) | copy-start | bytes 12292
  39.1 140.1 %copy-start.19 = (f32[1,1024]{1,0:T(1,128)}, f32[1,1024]{1,0:T(1,128)S(1)}, u32[]{:S(2)}) copy-start(f32[1,1024]{1,0:T(1,128)S(1)} %get-tuple-element.59) | copy-start | bytes 12292
  39.1 140.1 %copy-start.21 = (f32[1,1024]{1,0:T(1,128)}, f32[1,1024]{1,0:T(1,128)S(1)}, u32[]{:S(2)}) copy-start(f32[1,1024]{1,0:T(1,128)S(1)} %get-tuple-element.60) | copy-start | bytes 12292
  39.2 140.1 %copy-start.23 = (f32[1,1024]{1,0:T(1,128)}, f32[1,1024]{1,0:T(1,128)S(1)}, u32[]{:S(2)}) copy-start(f32[1,1024]{1,0:T(1,128)S(1)} %get-tuple-element.55) | copy-start | bytes 12292
  39.2 140.1 %copy-start.25 = (f32[1,1024]{1,0:T(1,128)}, f32[1,1024]{1,0:T(1,128)S(1)}, u32[]{:S(2)}) copy-start(f32[1,1024]{1,0:T(1,128)S(1)} %get-tuple-element.56) | copy-start | bytes 12292
  39.2 140.1 %copy-start.27 = (f32[1,1024]{1,0:T(1,128)}, f32[1,1024]{1,0:T(1,128)S(1)}, u32[]{:S(2)}) copy-start(f32[1,1024]{1,0:T(1,128)S(1)} %get-tuple-element.57) | copy-start | bytes 12292
  41.6 137.7 %copy-start.42 = (f32[128]{0:T(128)}, f32[128]{0:T(128)S(1)}, u32[]{:S(2)}) copy-start(f32[128]{0:T(128)S(1)} %pad_maximum_fusion.17) | copy-start | bytes 1540
  180.1 18.0 %collective-permute-start.2 = (f32[1,1024]{1,0:T(1,128)S(1)}, f32[1,1024]{1,0:T(1,128)S(1)}, u32[]{:S(2)}, u32[]{:S(2)}) collective-permute-start(f32[1,1024]{1,0:T(1,128)S(1)} %slice.515), channel_id=1, source_target_pairs={{4,0},{8,4},{12,8},{16,12},{20,16},{24,20},{28,24},{32,28},{36,32}... | collective-permute-start | bytes 12296 | tf_op jit(solution)/shard_map/ppermute | solution.py:32
  233.5 14.4 %copy-start.16 = (f32[3,1024]{1,0:T(4,128)S(1)}, f32[3,1024]{1,0:T(4,128)}, u32[]{:S(2)}) copy-start(f32[3,1024]{1,0:T(4,128)} %slice.446) | copy-start | bytes 36868
  265.6 25.2 %all-to-all-start.2 = ((f32[64,2,1024]{2,1,0:T(2,128)}), f32[64,2,1024]{2,1,0:T(2,128)}, u32[]{:S(2)}, u32[]{:S(2)}) async-start(f32[64,2,1024]{2,1,0:T(2,128)} %broadcast_in_dim.37), calls=%async_computation.2 | async-start | bytes 1048576 | tf_op jit(solution)/shard_map/all_to_all | solution.py:15
  273.4 185.7 %reduce-scatter.2.cloned.1.call-start = ((), (), s32[]{:S(2)}) async-start(), calls=%async_computation.5 | async-start | bytes 12779520 | tf_op jit(solution)/shard_map/reduce_scatter | solution.py:139
  301.8 63.1 %copy-start.5 = (bf16[128,1024]{1,0:T(8,128)(2,1)S(1)}, bf16[128,1024]{1,0:T(8,128)(2,1)}, u32[]{:S(2)}) copy-start(bf16[128,1024]{1,0:T(8,128)(2,1)} %copy-done.4) | copy-start | bytes 786436
  301.8 63.1 %copy-start.7 = (bf16[128,1024]{1,0:T(8,128)(2,1)S(1)}, bf16[128,1024]{1,0:T(8,128)(2,1)}, u32[]{:S(2)}) copy-start(bf16[128,1024]{1,0:T(8,128)(2,1)} %copy-done.6) | copy-start | bytes 786436
  301.8 63.1 %copy-start.9 = (bf16[128,1024]{1,0:T(8,128)(2,1)S(1)}, bf16[128,1024]{1,0:T(8,128)(2,1)}, u32[]{:S(2)}) copy-start(bf16[128,1024]{1,0:T(8,128)(2,1)} %copy-done.8) | copy-start | bytes 786436
  460.7 9.2 %all-to-all-start.3 = ((bf16[4,48,256]{2,1,0:T(8,128)(2,1)}), bf16[4,48,256]{2,1,0:T(8,128)(2,1)S(1)}, u32[]{:S(2)}, u32[]{:S(2)}) async-start(bf16[4,48,256]{2,1,0:T(8,128)(2,1)} %bitcast.46), calls=%async_computation.4 | async-start | bytes 196608 | tf_op jit(solution)/shard_map/all_to_all | solution.py:81
  (28 other events, 74.6 us)
Sparse Core Ops, SparseCore 0:
  301.9 157.1 reduce-scatter.1
